TPU v7x, 32 devices: a whole 2x2x4 slice. The times are simulated.
32 devices in a mesh: dap: 16 (over z, y, x), dp: 2 (over core).
Axes of the slice: x: 2, y: 2, z: 4, core: 2. Of those that a mesh axis runs over, the one named last changes fastest.
Arguments:
- edge_embedding: bfloat16 [192, 96, 128], P(('dp', 'dap')), parts along dimension 0, may hold values from -6 to 6
- alignment_embedding: bfloat16 [128, 96, 256], P('dp', 'dap'), parts along dimension 0, may hold values from -6 to 6
- tensor_flank_matrix: bfloat16 [256, 64], replicated, may hold values from -0.375 to 0.375
- tensor_final_matrix: bfloat16 [1024, 128], replicated, may hold values from -0.75 to 0.75
- outward_sigmoid_matrix: bfloat16 [128, 640], replicated, may hold values from -0.5 to 0.5
- outward_final_matrix: bfloat16 [128, 128], replicated, may hold values from -0.5 to 0.5
- inward_sigmoid_matrix: bfloat16 [128, 640], replicated, may hold values from -0.5 to 0.5
- inward_final_matrix: bfloat16 [128, 128], replicated, may hold values from -0.5 to 0.5
- adjoint_seed: bfloat16 [192, 96, 128], P(('dp', 'dap')), parts along dimension 0, may hold values from -6 to 6
Outputs:
- edge_embedding_updated: bfloat16 [192, 96, 128], P(('dp', 'dap')), parts along dimension 0
- edge_embedding_adjoint: bfloat16 [192, 96, 128], P(('dp', 'dap')), parts along dimension 0
- alignment_adjoint: bfloat16 [128, 96, 256], P('dp', 'dap'), parts along dimension 0
- outer_proj_grad: float32 [512, 64], P('dp'), parts along dimension 0
- outer_final_grad: float32 [2048, 128], P('dp'), parts along dimension 0
- outgoing_proj_grad: float32 [256, 640], P('dp'), parts along dimension 0
- outgoing_final_grad: float32 [256, 128], P('dp'), parts along dimension 0
- incoming_proj_grad: float32 [256, 640], P('dp'), parts along dimension 0
- incoming_final_grad: float32 [256, 128], P('dp'), parts along dimension 0
There are 2 independent parts, one for each index of `dp`. A program takes and returns all parts, laid end to end along the dimension named above; an argument that names none is the same for every part. Nothing has to cross between parts.
All inputs are finite; a program needn't handle non-finite values.
Results may differ from a plain program's by a relative error of at most 0.02.
Values may be sent and summed in bfloat16 or wider, within the bound.
No kernel may reach another device: no remote copies, remote signals or barrier semaphores. Data moves between devices by JAX's collectives and lax.ppermute only.
A program may use at most 128 MiB of HBM per device.

v0:
```python
import jax
import jax.numpy as jnp
from jax import lax
from jax.sharding import PartitionSpec as P

EPSILON = 1e-05


def truncated_numbers(values):
    return lax.optimization_barrier(values.astype(jnp.bfloat16))


def edge_standardized(values, which_axis):
    average = jnp.mean(values, axis=which_axis, keepdims=True)
    centred = values - average
    factor = lax.rsqrt(jnp.mean(centred * centred, axis=which_axis, keepdims=True) + EPSILON)
    return centred * factor


def standardizer_adjoint(values, gradient, which_axis):
    average = jnp.mean(values, axis=which_axis, keepdims=True)
    centred = values - average
    factor = lax.rsqrt(jnp.mean(centred * centred, axis=which_axis, keepdims=True) + EPSILON)
    hatted = centred * factor
    return factor * (
        gradient
        - jnp.mean(gradient, axis=which_axis, keepdims=True)
        - hatted * jnp.mean(gradient * hatted, axis=which_axis, keepdims=True)
    )


def sigmoid_pieces(edge_entry, linear_mapping, latent_tensor):
    standardized_edges = truncated_numbers(edge_standardized(edge_entry.astype(jnp.float32), 2))
    gate_pre = jnp.dot(
        standardized_edges,
        linear_mapping[:, 4 * latent_tensor :],
        preferred_element_type=jnp.float32,
    )
    split_pre = jnp.einsum(
        "rnz,zc->crn",
        standardized_edges,
        linear_mapping[:, : 4 * latent_tensor],
        preferred_element_type=jnp.float32,
    )
    source_masked = truncated_numbers(
        jax.nn.sigmoid(split_pre[:latent_tensor]) * split_pre[latent_tensor : 2 * latent_tensor]
    )
    target_masked = truncated_numbers(
        jax.nn.sigmoid(split_pre[2 * latent_tensor : 3 * latent_tensor])
        * split_pre[3 * latent_tensor :]
    )
    return (standardized_edges, gate_pre, split_pre, source_masked, target_masked)


def grouped(values, groups):
    return values.reshape((groups, values.shape[0] // groups) + values.shape[1:])


def gathered(values, axis):
    groups = lax.axis_size("dap")
    copies = jnp.broadcast_to(values[None], (groups,) + values.shape)
    return jnp.moveaxis(lax.all_to_all(copies, "dap", 0, 0, tiled=True), 0, axis)


def exchanged(values):
    return lax.all_to_all(values, "dap", split_axis=0, concat_axis=0, tiled=True)


def totalled(parts):
    groups = lax.axis_size("dap")
    flat = jnp.concatenate([part.reshape(-1) for part in parts])
    unit = groups * 16 * 128
    padded = -(-flat.size // unit) * unit
    blocks = jnp.pad(flat, (0, padded - flat.size)).reshape(groups, -1, 128)
    mine = exchanged(truncated_numbers(blocks)).astype(jnp.float32).sum(axis=0)
    whole = gathered(truncated_numbers(mine), 0).astype(jnp.float32).reshape(-1)
    out, place = ([], 0)
    for part in parts:
        out.append(whole[place : place + part.size].reshape(part.shape))
        place += part.size
    return out


def to_channels(*rows):
    groups = lax.axis_size("dap")
    packed = jnp.stack([grouped(values, groups) for values in rows], axis=1)
    received = exchanged(packed)
    return [
        jnp.moveaxis(received[:, at], 0, 1).reshape(received.shape[2], -1, received.shape[4])[None]
        for at in range(len(rows))
    ]


def to_rows(*columns):
    groups = lax.axis_size("dap")
    packed = jnp.stack(
        [
            jnp.moveaxis(values[0].reshape(values.shape[1], groups, -1, values.shape[3]), 1, 0)
            for values in columns
        ],
        axis=1,
    )
    received = exchanged(packed)
    return [received[:, at].reshape((-1,) + received.shape[3:]) for at in range(len(columns))]


def contract_items(left_cols, right_cols, outgoing):
    if outgoing:
        return jnp.einsum(
            "xqik,xqjk->xqij", left_cols, right_cols, preferred_element_type=jnp.float32
        )
    return jnp.einsum("xqki,xqkj->xqij", left_cols, right_cols, preferred_element_type=jnp.float32)


def contract_back_items(grad_cols, left_cols, right_cols, outgoing):
    if outgoing:
        source_adjoint = jnp.einsum(
            "xqij,xqjk->xqik", grad_cols, right_cols, preferred_element_type=jnp.float32
        )
        target_adjoint = jnp.einsum(
            "xqij,xqik->xqjk", grad_cols, left_cols, preferred_element_type=jnp.float32
        )
    else:
        source_adjoint = jnp.einsum(
            "xqij,xqkj->xqki", grad_cols, right_cols, preferred_element_type=jnp.float32
        )
        target_adjoint = jnp.einsum(
            "xqij,xqki->xqkj", grad_cols, left_cols, preferred_element_type=jnp.float32
        )
    return (truncated_numbers(source_adjoint), truncated_numbers(target_adjoint))


def triangle_forward(edge_entry, linear_mapping, final, outgoing):
    latent_tensor = final.shape[0]
    groups = lax.axis_size("dap")
    standardized_edges, gate_pre, split_pre, source_masked, target_masked = sigmoid_pieces(
        edge_entry, linear_mapping, latent_tensor
    )
    kept = to_channels(source_masked, target_masked)
    triangle_cols = truncated_numbers(contract_items(kept[0], kept[1], outgoing))
    (triangle,) = to_rows(triangle_cols)
    unit_norm = truncated_numbers(edge_standardized(triangle.astype(jnp.float32), 0))
    values = jnp.einsum("crn,cz->rnz", unit_norm, final, preferred_element_type=jnp.float32)
    pair_new = truncated_numbers(edge_entry.astype(jnp.float32) + jax.nn.sigmoid(gate_pre) * values)
    return (pair_new, triangle, kept)


def triangle_back(edge_entry, linear_mapping, final, outgoing, triangle, kept, gradient):
    latent_tensor = final.shape[0]
    groups = lax.axis_size("dap")
    standardized_edges, gate_pre, split_pre, source_masked, target_masked = sigmoid_pieces(
        edge_entry, linear_mapping, latent_tensor
    )
    sigmoid_factor = jax.nn.sigmoid(gate_pre)
    tri_wide = triangle.astype(jnp.float32)
    unit_norm = truncated_numbers(edge_standardized(tri_wide, 0))
    values = jnp.einsum("crn,cz->rnz", unit_norm, final, preferred_element_type=jnp.float32)
    scaled = truncated_numbers(gradient * sigmoid_factor)
    final_sum = jnp.einsum("crn,rnz->cz", unit_norm, scaled, preferred_element_type=jnp.float32)
    grad_unit = jnp.einsum("rnz,cz->crn", scaled, final, preferred_element_type=jnp.float32)
    adjoint_sigmoid = truncated_numbers(gradient * values * sigmoid_factor * (1.0 - sigmoid_factor))
    grad_triangle = truncated_numbers(standardizer_adjoint(tri_wide, grad_unit, 0))
    (gradient_cols,) = to_channels(grad_triangle)
    left_back, right_back = contract_back_items(gradient_cols, kept[0], kept[1], outgoing)
    source_adjoint, target_adjoint = [
        values.astype(jnp.float32) for values in to_rows(left_back, right_back)
    ]
    logistic_primary = jax.nn.sigmoid(split_pre[:latent_tensor])
    logistic_tertiary = jax.nn.sigmoid(split_pre[2 * latent_tensor : 3 * latent_tensor])
    grad_split = truncated_numbers(
        jnp.concatenate(
            [
                source_adjoint
                * split_pre[latent_tensor : 2 * latent_tensor]
                * logistic_primary
                * (1.0 - logistic_primary),
                source_adjoint * logistic_primary,
                target_adjoint
                * split_pre[3 * latent_tensor :]
                * logistic_tertiary
                * (1.0 - logistic_tertiary),
                target_adjoint * logistic_tertiary,
            ],
            axis=0,
        )
    )
    proj_sum = jnp.concatenate(
        [
            jnp.einsum(
                "rnz,crn->zc", standardized_edges, grad_split, preferred_element_type=jnp.float32
            ),
            jnp.einsum(
                "rnz,rnc->zc",
                standardized_edges,
                adjoint_sigmoid,
                preferred_element_type=jnp.float32,
            ),
        ],
        axis=1,
    )
    grad_norm = jnp.einsum(
        "crn,zc->rnz",
        grad_split,
        linear_mapping[:, : 4 * latent_tensor],
        preferred_element_type=jnp.float32,
    )
    grad_norm = grad_norm + jnp.dot(
        adjoint_sigmoid,
        linear_mapping[:, 4 * latent_tensor :].T,
        preferred_element_type=jnp.float32,
    )
    grad_pair = gradient + standardizer_adjoint(edge_entry.astype(jnp.float32), grad_norm, 2)
    return (grad_pair, proj_sum, final_sum)


def shards(
    edge_embedding,
    alignment_embedding,
    tensor_flank_matrix,
    tensor_final_matrix,
    outward_sigmoid_matrix,
    outward_final_matrix,
    inward_sigmoid_matrix,
    inward_final_matrix,
    adjoint_seed,
):
    rows_here = edge_embedding.shape[0]
    residues = edge_embedding.shape[1]
    alignment_depth = alignment_embedding.shape[0]
    contraction_extent = tensor_flank_matrix.shape[1] // 2
    alignment_standardized = truncated_numbers(
        edge_standardized(alignment_embedding.astype(jnp.float32), 2)
    )
    alignment_mapped = jnp.dot(
        alignment_standardized, tensor_flank_matrix, preferred_element_type=jnp.float32
    )
    tensor_source_factor = truncated_numbers(alignment_mapped[..., :contraction_extent])
    tensor_target_factor = truncated_numbers(alignment_mapped[..., contraction_extent:])
    right_all = gathered(tensor_target_factor, 1).reshape(
        alignment_depth, residues, contraction_extent
    )
    tile_lines = 128 if residues % 128 == 0 else residues
    tile_number = residues // tile_lines
    outer_parts = []
    first_parts = []
    for block_index in range(tile_number):
        lower = block_index * tile_lines
        right_block = right_all[:, lower : lower + tile_lines]
        triangle_contraction = jnp.einsum(
            "sic,sjd->ijcd", tensor_source_factor, right_block, preferred_element_type=jnp.float32
        )
        outer_block = truncated_numbers(
            triangle_contraction.reshape(
                rows_here, tile_lines, contraction_extent * contraction_extent
            )
            / alignment_depth
        )
        update = jnp.dot(outer_block, tensor_final_matrix, preferred_element_type=jnp.float32)
        first_parts.append(
            truncated_numbers(
                edge_embedding[:, lower : lower + tile_lines].astype(jnp.float32) + update
            )
        )
        outer_parts.append(outer_block)
    outer_mean = jnp.concatenate(outer_parts, axis=1)
    pair_one = jnp.concatenate(first_parts, axis=1)
    pair_two, triangle_out, kept_out = triangle_forward(
        pair_one, outward_sigmoid_matrix, outward_final_matrix, True
    )
    edge_embedding_updated, triangle_in, kept_in = triangle_forward(
        pair_two, inward_sigmoid_matrix, inward_final_matrix, False
    )
    grad_two, inward_sigmoid_accrual, inward_final_accrual = triangle_back(
        pair_two,
        inward_sigmoid_matrix,
        inward_final_matrix,
        False,
        triangle_in,
        kept_in,
        adjoint_seed.astype(jnp.float32),
    )
    grad_one, outward_sigmoid_accrual, outward_final_accrual = triangle_back(
        pair_one,
        outward_sigmoid_matrix,
        outward_final_matrix,
        True,
        triangle_out,
        kept_out,
        grad_two,
    )
    edge_embedding_adjoint = truncated_numbers(grad_one)
    tensor_final_accrual = jnp.einsum(
        "rnk,rnz->kz", outer_mean, edge_embedding_adjoint, preferred_element_type=jnp.float32
    )
    source_adjoint = jnp.zeros((alignment_depth, rows_here, contraction_extent), jnp.float32)
    outer_grads = []
    for block_index in range(tile_number):
        lower = block_index * tile_lines
        right_block = right_all[:, lower : lower + tile_lines]
        adjoint_tensor_mean = truncated_numbers(
            jnp.dot(
                edge_embedding_adjoint[:, lower : lower + tile_lines],
                tensor_final_matrix.T,
                preferred_element_type=jnp.float32,
            )
        )
        adjoint_tensor_mean = adjoint_tensor_mean.reshape(
            rows_here, tile_lines, contraction_extent, contraction_extent
        )
        source_adjoint = (
            source_adjoint
            + jnp.einsum(
                "mopz,loz->lmp",
                adjoint_tensor_mean,
                right_block,
                preferred_element_type=jnp.float32,
            )
            / alignment_depth
        )
        outer_grads.append(adjoint_tensor_mean)
    pair_columns = lax.all_to_all(
        edge_embedding_adjoint, "dap", split_axis=1, concat_axis=0, tiled=True
    )
    left_all = gathered(tensor_source_factor, 1).reshape(
        alignment_depth, residues, contraction_extent
    )
    target_adjoint = jnp.zeros((alignment_depth, rows_here, contraction_extent), jnp.float32)
    for block_index in range(tile_number):
        lower = block_index * tile_lines
        column_grad = truncated_numbers(
            jnp.dot(
                pair_columns[lower : lower + tile_lines],
                tensor_final_matrix.T,
                preferred_element_type=jnp.float32,
            )
        )
        column_grad = column_grad.reshape(
            tile_lines, rows_here, contraction_extent, contraction_extent
        )
        target_adjoint = (
            target_adjoint
            + jnp.einsum(
                "gxqp,vgq->vxp",
                column_grad,
                left_all[:, lower : lower + tile_lines],
                preferred_element_type=jnp.float32,
            )
            / alignment_depth
        )
    alignment_mapped_adjoint = truncated_numbers(
        jnp.concatenate([source_adjoint, target_adjoint], axis=2)
    )
    tensor_flank_accrual = jnp.einsum(
        "ajo,ajm->om",
        alignment_standardized,
        alignment_mapped_adjoint,
        preferred_element_type=jnp.float32,
    )
    alignment_standard_adjoint = jnp.dot(
        alignment_mapped_adjoint, tensor_flank_matrix.T, preferred_element_type=jnp.float32
    )
    alignment_adjoint = truncated_numbers(
        standardizer_adjoint(alignment_embedding.astype(jnp.float32), alignment_standard_adjoint, 2)
    )
    totals = totalled(
        (
            tensor_flank_accrual,
            tensor_final_accrual,
            outward_sigmoid_accrual,
            outward_final_accrual,
            inward_sigmoid_accrual,
            inward_final_accrual,
        )
    )
    return (
        edge_embedding_updated,
        edge_embedding_adjoint,
        alignment_adjoint,
        totals[0] / residues,
        totals[1] / residues,
        totals[2] / residues,
        totals[3] / residues,
        totals[4] / residues,
        totals[5] / residues,
    )


def solution(mesh):
    placed = (
        P(("dp", "dap"), None, None),
        P("dp", "dap", None),
        P(),
        P(),
        P(),
        P(),
        P(),
        P(),
        P(("dp", "dap"), None, None),
    )
    return jax.shard_map(
        shards,
        mesh=mesh,
        in_specs=placed,
        out_specs=(
            P(("dp", "dap"), None, None),
            P(("dp", "dap"), None, None),
            P("dp", "dap", None),
            P("dp", None),
            P("dp", None),
            P("dp", None),
            P("dp", None),
            P("dp", None),
            P("dp", None),
        ),
        check_vma=False,
    )
```

profile of v0, /device:TPU:0, one launch (start us, length us, event | category | flops | bytes accessed | tf_op | source)
XLA Modules:
  0.0 255.0 jit_solution(16639720308278416110)
XLA Ops:
  0.7 1.1 convert_reduce_fusion
  1.8 1.2 fusion.53
  3.0 1.1 fusion.48
  4.1 1.0 convolution_convert_fusion.8
  5.3 1.3 reshape.289
  6.6 8.3 %all-to-all-start = ((bf16[16,2,6144]{2,1,0:T(2,128)(2,1)}), bf16[16,2,6144]{2,1,0:T(2,128)(2,1)S(1)}, u32[]{:S(2)}, u32[]{:S(2)}) async-start(bf16[16,2,6144]{2,1,0:T(2,128)(2,1)} %reshape.289), calls=%async_computation | async-start | bytes 786432 | tf_op jit(solution)/shard_map/all_to_all | solution.py:62
  14.9 12.6 %all-to-all-done = bf16[16,2,6144]{2,1,0:T(2,128)(2,1)S(1)} async-done(((bf16[16,2,6144]{2,1,0:T(2,128)(2,1)}), bf16[16,2,6144]{2,1,0:T(2,128)(2,1)S(1)}, u32[]{:S(2)}, u32[]{:S(2)}) %all-to-all-start) | async-done | bytes 393248 | tf_op jit(solution)/shard_map/all_to_all | solution.py:62
  28.1 0.8 fusion.2
  28.9 1.0 copy.171
  32.4 15.4 %all_to_all.78 = bf16[16,2,8,6,96]{4,2,3,1,0:T(8,128)(2,1)S(1)} all-to-all(bf16[16,2,8,6,96]{4,2,3,1,0:T(8,128)(2,1)S(1)} %copy.175), channel_id=1, replica_groups=mesh['dap'=16,'dp'=2] {'dap'}, dimensions={0} | all-to-all | bytes 589824 | tf_op jit(solution)/shard_map/all_to_all | solution.py:66
  48.5 11.5 %all_to_all.79 = bf16[16,1,8,6,96]{4,2,3,1,0:T(8,128)(2,1)S(1)} all-to-all(bf16[16,1,8,6,96]{4,2,3,1,0:T(8,128)(2,1)S(1)} %bitcast.340), channel_id=1, replica_groups=mesh['dap'=16,'dp'=2] {'dap'}, dimensions={0} | all-to-all | bytes 294912 | tf_op jit(solution)/shard_map/all_to_all | solution.py:66
  61.5 1.8 fusion.74
  65.8 0.9 multiply_convert_fusion.14
  66.7 1.7 copy.185
  68.4 1.7 copy.184
  70.1 1.1 pad_maximum_fusion.3
  71.3 13.2 %all_to_all.80 = bf16[16,2,8,6,96]{4,2,3,1,0:T(8,128)(2,1)S(1)} all-to-all(bf16[16,2,8,6,96]{4,2,3,1,0:T(8,128)(2,1)S(1)} %copy.186), channel_id=1, replica_groups=mesh['dap'=16,'dp'=2] {'dap'}, dimensions={0} | all-to-all | bytes 589824 | tf_op jit(solution)/shard_map/all_to_all | solution.py:66
  85.3 11.8 %all_to_all.81 = bf16[16,1,8,6,96]{4,2,3,1,0:T(8,128)(2,1)S(1)} all-to-all(bf16[16,1,8,6,96]{4,2,3,1,0:T(8,128)(2,1)S(1)} %bitcast.341), channel_id=1, replica_groups=mesh['dap'=16,'dp'=2] {'dap'}, dimensions={0} | all-to-all | bytes 294912 | tf_op jit(solution)/shard_map/all_to_all | solution.py:66
  98.5 1.9 copy.194
  100.3 1.0 convert_reduce_fusion.3
  101.3 1.0 multiply_reduce_fusion
  102.4 1.2 fusion.96
  103.6 1.0 fusion.119
  104.6 2.1 fusion.79
  107.4 1.0 multiply_convert_fusion.12
  108.4 1.7 copy.195
  110.1 1.0 copy.196
  111.1 11.1 %all_to_all.82 = bf16[16,1,8,6,96]{4,2,3,1,0:T(8,128)(2,1)S(1)} all-to-all(bf16[16,1,8,6,96]{4,2,3,1,0:T(8,128)(2,1)S(1)} %copy.196), channel_id=1, replica_groups=mesh['dap'=16,'dp'=2] {'dap'}, dimensions={0} | all-to-all | bytes 294912 | tf_op jit(solution)/shard_map/all_to_all | solution.py:66
  122.2 1.1 fusion.16
  124.7 4.4 %all-to-all-start.6 = ((bf16[16,2,8,6,96]{4,2,3,1,0:T(8,128)(2,1)}), bf16[16,2,8,6,96]{4,2,3,1,0:T(8,128)(2,1)}, u32[]{:S(2)}, u32[]{:S(2)}) async-start(bf16[16,2,8,6,96]{4,2,3,1,0:T(8,128)(2,1)} %copy.203), calls=%async_computation.6 | async-start | bytes 786432 | tf_op jit(solution)/shard_map/all_to_all | solution.py:66
  129.1 1.8 broadcast_bitcast_fusion
  130.9 2.7 %reshape.291 = bf16[16,2,6144]{2,1,0:T(2,128)(2,1)} reshape(bf16[16,6,32,64]{3,2,1,0:T(8,128)(2,1)} %broadcast_bitcast_fusion) | data formatting | bytes 786432
  133.6 4.9 %all-to-all-done.6 = bf16[16,2,8,6,96]{4,2,3,1,0:T(8,128)(2,1)} async-done(((bf16[16,2,8,6,96]{4,2,3,1,0:T(8,128)(2,1)}), bf16[16,2,8,6,96]{4,2,3,1,0:T(8,128)(2,1)}, u32[]{:S(2)}, u32[]{:S(2)}) %all-to-all-start.6) | async-done | bytes 294944 | tf_op jit(solution)/shard_map/all_to_all | solution.py:66
  138.6 4.2 %all-to-all-start.9 = ((bf16[16,2,6144]{2,1,0:T(2,128)(2,1)}), bf16[16,2,6144]{2,1,0:T(2,128)(2,1)}, u32[]{:S(2)}, u32[]{:S(2)}) async-start(bf16[16,2,6144]{2,1,0:T(2,128)(2,1)} %reshape.291), calls=%async_computation.9 | async-start | bytes 786432 | tf_op jit(solution)/shard_map/all_to_all | solution.py:62
  142.8 1.8 slice_convert_fusion.3
  145.4 1.9 copy.205
  147.2 1.8 copy.295
  149.0 1.9 copy.208
  150.9 1.3 multiply_convert_fusion.11
  153.8 1.1 multiply_convert_fusion.1
  157.4 6.9 %all-to-all-start.7 = ((bf16[16,1,8,6,96]{4,2,3,1,0:T(8,128)(2,1)}), bf16[16,1,8,6,96]{4,2,3,1,0:T(8,128)(2,1)}, u32[]{:S(2)}, u32[]{:S(2)}) async-start(bf16[16,1,8,6,96]{4,2,3,1,0:T(8,128)(2,1)} %copy.211), calls=%async_computation.7 | async-start | bytes 393216 | tf_op jit(solution)/shard_map/all_to_all | solution.py:66
  164.3 2.7 %reshape.292 = bf16[16,6,32,64]{3,2,1,0:T(8,128)(2,1)} reshape(bf16[16,2,6144]{2,1,0:T(2,128)(2,1)} %all-to-all-done.9) | data formatting | bytes 786432
  167.0 2.7 %copy.232 = bf16[64,96,32]{1,0,2:T(8,128)(2,1)} copy(bf16[64,96,32]{0,2,1:T(8,128)(2,1)} %bitcast.322) | data formatting | bytes 786432 | tf_op jit(solution)/shard_map/reshape | solution.py:324
  169.7 1.6 copy.226
  171.3 0.9 fusion.36
  172.4 1.1 copy.215
  173.5 1.1 fusion.18
  176.0 6.7 %all-to-all-start.8 = ((bf16[16,2,8,6,96]{4,2,3,1,0:T(8,128)(2,1)}), bf16[16,2,8,6,96]{4,2,3,1,0:T(8,128)(2,1)S(1)}, u32[]{:S(2)}, u32[]{:S(2)}) async-start(bf16[16,2,8,6,96]{4,2,3,1,0:T(8,128)(2,1)} %copy.218), calls=%async_computation.8 | async-start | bytes 786432 | tf_op jit(solution)/shard_map/all_to_all | solution.py:66
  183.8 0.9 fusion.32
  184.6 7.6 %all-to-all-done.8 = bf16[16,2,8,6,96]{4,2,3,1,0:T(8,128)(2,1)S(1)} async-done(((bf16[16,2,8,6,96]{4,2,3,1,0:T(8,128)(2,1)}), bf16[16,2,8,6,96]{4,2,3,1,0:T(8,128)(2,1)S(1)}, u32[]{:S(2)}, u32[]{:S(2)}) %all-to-all-start.8) | async-done | bytes 294944 | tf_op jit(solution)/shard_map/all_to_all | solution.py:66
  196.4 3.8 %all-to-all-start.10 = ((bf16[6,96,128]{2,0,1:T(8,128)(2,1)}), bf16[6,96,128]{2,0,1:T(8,128)(2,1)S(1)}, u32[]{:S(2)}, u32[]{:S(2)}) async-start(bf16[6,96,128]{2,0,1:T(8,128)(2,1)} %copy.228), calls=%async_computation.10 | async-start | bytes 393216 | tf_op jit(solution)/shard_map/all_to_all | solution.py:321
  200.2 1.6 copy.225
  202.6 2.6 %fusion.28 = bf16[64,6,32]{0,2,1:T(8,128)(2,1)} fusion(bf16[6,96,32,32]{1,3,2,0:T(8,128)(2,1)} %bitcast.338, bf16[64,96,32]{1,0,2:T(8,128)(2,1)S(1)} %copy-done.46), kind=kOutput, calls=%fused_computation.47 | convolution fusion | flops 75522048 | bytes 1597440 | tf_op jit(solution)/shard_map/mopz,loz->lmp/dot_general | solution.py:312
  205.3 3.0 %all-to-all-done.10 = bf16[6,96,128]{2,0,1:T(8,128)(2,1)S(1)} async-done(((bf16[6,96,128]{2,0,1:T(8,128)(2,1)}), bf16[6,96,128]{2,0,1:T(8,128)(2,1)S(1)}, u32[]{:S(2)}, u32[]{:S(2)}) %all-to-all-start.10) | async-done | bytes 147488 | tf_op jit(solution)/shard_map/all_to_all | solution.py:321
  208.9 0.9 copy.231
  209.8 1.7 fusion.31
  213.4 17.6 %all_to_all.83 = bf16[16,176,128]{2,1,0:T(8,128)(2,1)S(1)} all-to-all(bf16[16,176,128]{2,1,0:T(8,128)(2,1)S(1)} %bitcast.323), channel_id=1, replica_groups=mesh['dap'=16,'dp'=2] {'dap'}, dimensions={0} | all-to-all | bytes 1441792 | tf_op jit(solution)/shard_map/all_to_all | solution.py:66
  231.1 1.0 broadcast_in_dim.8
  232.1 3.6 %all-to-all-start.12 = ((bf16[16,176,128]{2,1,0:T(8,128)(2,1)}), bf16[16,176,128]{2,1,0:T(8,128)(2,1)S(1)}, u32[]{:S(2)}, u32[]{:S(2)}) async-start(bf16[16,176,128]{2,1,0:T(8,128)(2,1)} %broadcast_in_dim.8), calls=%async_computation.12 | async-start | bytes 1441792 | tf_op jit(solution)/shard_map/all_to_all | solution.py:62
  236.1 1.0 fusion.52
  237.1 11.2 %all-to-all-done.12 = bf16[16,176,128]{2,1,0:T(8,128)(2,1)S(1)} async-done(((bf16[16,176,128]{2,1,0:T(8,128)(2,1)}), bf16[16,176,128]{2,1,0:T(8,128)(2,1)S(1)}, u32[]{:S(2)}, u32[]{:S(2)}) %all-to-all-start.12) | async-done | bytes 720928 | tf_op jit(solution)/shard_map/all_to_all | solution.py:62
  248.4 0.8 slice_multiply_fusion
  249.9 1.8 slice.132
  251.7 0.9 slice_multiply_fusion.3
  (258 shorter events, 29.7 us)
Async XLA Ops:
  0.6 29.3 %copy-start = (bf16[1024,128]{1,0:T(8,128)(2,1)S(1)}, bf16[1024,128]{1,0:T(8,128)(2,1)}, u32[]{:S(2)}) copy-start(bf16[1024,128]{1,0:T(8,128)(2,1)} %param.12) | copy-start | bytes 786436
  1.8 3.3 %copy-start.56 = (f32[64,6]{0,1:T(8,128)}, f32[64,6]{0,1:T(8,128)S(1)}, u32[]{:S(2)}) copy-start(f32[64,6]{0,1:T(8,128)S(1)} %broadcast_multiply_fusion.14) | copy-start | bytes 4612
  3.0 2.2 copy-start.64
  4.1 1.1 copy-start.16
  5.1 22.9 %copy-start.47 = (bf16[64,6,32]{0,2,1:T(8,128)(2,1)}, bf16[64,6,32]{0,2,1:T(8,128)(2,1)S(1)}, u32[]{:S(2)}) copy-start(bf16[64,6,32]{0,2,1:T(8,128)(2,1)S(1)} %get-tuple-element.79) | copy-start | bytes 73732
  6.6 21.0 %all-to-all-start = ((bf16[16,2,6144]{2,1,0:T(2,128)(2,1)}), bf16[16,2,6144]{2,1,0:T(2,128)(2,1)S(1)}, u32[]{:S(2)}, u32[]{:S(2)}) async-start(bf16[16,2,6144]{2,1,0:T(2,128)(2,1)} %reshape.289), calls=%async_computation | async-start | bytes 786432 | tf_op jit(solution)/shard_map/all_to_all | solution.py:62
  28.9 1.1 copy-start.48
  29.9 1.2 copy-start.1
  29.9 1.4 copy-start.44
  30.7 1.1 copy-start.58
  31.3 30.2 %copy-start.12 = (bf16[6,96,128]{2,1,0:T(8,128)(2,1)}, bf16[6,96,128]{2,1,0:T(8,128)(2,1)S(1)}, u32[]{:S(2)}) copy-start(bf16[6,96,128]{2,1,0:T(8,128)(2,1)S(1)} %fusion.58) | copy-start | bytes 442372
  47.9 12.2 %copy-start.18 = (bf16[16,1,8,6,96]{4,2,3,1,0:T(8,128)(2,1)}, bf16[16,1,8,6,96]{4,2,3,1,0:T(8,128)(2,1)S(1)}, u32[]{:S(2)}) copy-start(bf16[16,1,8,6,96]{4,2,3,1,0:T(8,128)(2,1)S(1)} %get-tuple-element.78) | copy-start | bytes 442372
  48.1 13.2 %copy-start.54 = (bf16[128,128]{1,0:T(8,128)(2,1)S(1)}, bf16[128,128]{1,0:T(8,128)(2,1)}, u32[]{:S(2)}) copy-start(bf16[128,128]{1,0:T(8,128)(2,1)} %param.14) | copy-start | bytes 98308
  60.2 3.0 %copy-start.4 = (f32[128,6,96]{0,2,1:T(8,128)}, f32[128,6,96]{0,2,1:T(8,128)S(1)}, u32[]{:S(2)}) copy-start(f32[128,6,96]{0,2,1:T(8,128)S(1)} %copy.183) | copy-start | bytes 884740
  60.3 3.4 %copy-start.60 = (f32[6,96]{1,0:T(8,128)}, f32[6,96]{1,0:T(8,128)S(1)}, u32[]{:S(2)}) copy-start(f32[6,96]{1,0:T(8,128)S(1)} %broadcast_multiply_fusion.10) | copy-start | bytes 6916
  60.4 3.3 %copy-start.68 = (f32[6,96]{1,0:T(8,128)}, f32[6,96]{1,0:T(8,128)S(1)}, u32[]{:S(2)}) copy-start(f32[6,96]{1,0:T(8,128)S(1)} %add_rsqrt_fusion.2) | copy-start | bytes 6916
  61.3 4.2 %copy-start.42 = (bf16[128,640]{1,0:T(8,128)(2,1)S(1)}, bf16[128,640]{1,0:T(8,128)(2,1)}, u32[]{:S(2)}) copy-start(bf16[128,640]{1,0:T(8,128)(2,1)} %param.15) | copy-start | bytes 491524
  61.5 2.3 copy-start.33
  102.3 4.3 %copy-start.6 = (f32[128,6,96]{0,2,1:T(8,128)S(1)}, f32[128,6,96]{0,2,1:T(8,128)}, u32[]{:S(2)}) copy-start(f32[128,6,96]{0,2,1:T(8,128)} %copy.194) | copy-start | bytes 884740
  102.4 4.3 %copy-start.53 = (bf16[128,128]{1,0:T(8,128)(2,1)S(1)}, bf16[128,128]{1,0:T(8,128)(2,1)}, u32[]{:S(2)}) copy-start(bf16[128,128]{1,0:T(8,128)(2,1)} %param.16) | copy-start | bytes 98308
  103.6 3.6 %copy-start.29 = (bf16[128,6,96]{0,2,1:T(8,128)(2,1)}, bf16[128,6,96]{0,2,1:T(8,128)(2,1)S(1)}, u32[]{:S(2)}) copy-start(bf16[128,6,96]{0,2,1:T(8,128)(2,1)S(1)} %fusion.96) | copy-start | bytes 442372
  110.1 13.3 %copy-start.22 = (bf16[16,1,8,6,96]{4,2,3,1,0:T(8,128)(2,1)S(1)}, bf16[16,1,8,6,96]{4,2,3,1,0:T(8,128)(2,1)}, u32[]{:S(2)}) copy-start(bf16[16,1,8,6,96]{4,2,3,1,0:T(8,128)(2,1)} %copy-done.21) | copy-start | bytes 442372
  124.7 13.9 %all-to-all-start.6 = ((bf16[16,2,8,6,96]{4,2,3,1,0:T(8,128)(2,1)}), bf16[16,2,8,6,96]{4,2,3,1,0:T(8,128)(2,1)}, u32[]{:S(2)}, u32[]{:S(2)}) async-start(bf16[16,2,8,6,96]{4,2,3,1,0:T(8,128)(2,1)} %copy.203), calls=%async_computation.6 | async-start | bytes 786432 | tf_op jit(solution)/shard_map/all_to_all | solution.py:66
  138.6 18.8 %all-to-all-start.9 = ((bf16[16,2,6144]{2,1,0:T(2,128)(2,1)}), bf16[16,2,6144]{2,1,0:T(2,128)(2,1)}, u32[]{:S(2)}, u32[]{:S(2)}) async-start(bf16[16,2,6144]{2,1,0:T(2,128)(2,1)} %reshape.291), calls=%async_computation.9 | async-start | bytes 786432 | tf_op jit(solution)/shard_map/all_to_all | solution.py:62
  150.9 1.5 copy-start.43
  152.2 1.0 copy-start.38
  152.2 1.0 copy-start.63
  152.2 1.0 copy-start.71
  152.3 1.5 copy-start.34
  152.3 1.5 copy-start.35
  152.3 1.5 copy-start.49
  153.2 2.4 copy-start.5
  153.2 2.4 copy-start.55
  153.2 2.4 copy-start.61
  153.2 2.4 copy-start.69
  155.6 11.4 %copy-start.31 = (bf16[6,96,128]{2,1,0:T(8,128)(2,1)}, bf16[6,96,128]{2,1,0:T(8,128)(2,1)S(1)}, u32[]{:S(2)}) copy-start(bf16[6,96,128]{2,1,0:T(8,128)(2,1)S(1)} %multiply_convert_fusion.7) | copy-start | bytes 442372
  157.4 15.0 %all-to-all-start.7 = ((bf16[16,1,8,6,96]{4,2,3,1,0:T(8,128)(2,1)}), bf16[16,1,8,6,96]{4,2,3,1,0:T(8,128)(2,1)}, u32[]{:S(2)}, u32[]{:S(2)}) async-start(bf16[16,1,8,6,96]{4,2,3,1,0:T(8,128)(2,1)} %copy.211), calls=%async_computation.7 | async-start | bytes 393216 | tf_op jit(solution)/shard_map/all_to_all | solution.py:66
  167.0 4.4 %copy-start.15 = (bf16[6,96,128]{2,1,0:T(8,128)(2,1)S(1)}, bf16[6,96,128]{2,1,0:T(8,128)(2,1)}, u32[]{:S(2)}) copy-start(bf16[6,96,128]{2,1,0:T(8,128)(2,1)} %copy-done.14) | copy-start | bytes 442372
  167.0 4.4 %copy-start.39 = (bf16[6,96,128]{2,1,0:T(8,128)(2,1)S(1)}, bf16[6,96,128]{2,1,0:T(8,128)(2,1)}, u32[]{:S(2)}) copy-start(bf16[6,96,128]{2,1,0:T(8,128)(2,1)} %get-tuple-element.68) | copy-start | bytes 442372
  169.7 4.9 %copy-start.19 = (bf16[16,1,8,6,96]{4,2,3,1,0:T(8,128)(2,1)S(1)}, bf16[16,1,8,6,96]{4,2,3,1,0:T(8,128)(2,1)}, u32[]{:S(2)}) copy-start(bf16[16,1,8,6,96]{4,2,3,1,0:T(8,128)(2,1)} %copy-done.18) | copy-start | bytes 442372
  175.1 7.9 %copy-start.52 = (bf16[128,128]{1,0:T(8,128)(2,1)S(1)}, bf16[128,128]{1,0:T(8,128)(2,1)}, u32[]{:S(2)}) copy-start(bf16[128,128]{1,0:T(8,128)(2,1)} %fusion.36) | copy-start | bytes 98308
  175.2 8.6 %copy-start.13 = (bf16[6,96,128]{2,1,0:T(8,128)(2,1)S(1)}, bf16[6,96,128]{2,1,0:T(8,128)(2,1)}, u32[]{:S(2)}) copy-start(bf16[6,96,128]{2,1,0:T(8,128)(2,1)} %copy-done.12) | copy-start | bytes 442372
  175.2 8.6 %copy-start.24 = (bf16[6,96,128]{2,1,0:T(8,128)(2,1)S(1)}, bf16[6,96,128]{2,1,0:T(8,128)(2,1)}, u32[]{:S(2)}) copy-start(bf16[6,96,128]{2,1,0:T(8,128)(2,1)} %get-tuple-element.46) | copy-start | bytes 442372
  176.0 16.3 %all-to-all-start.8 = ((bf16[16,2,8,6,96]{4,2,3,1,0:T(8,128)(2,1)}), bf16[16,2,8,6,96]{4,2,3,1,0:T(8,128)(2,1)S(1)}, u32[]{:S(2)}, u32[]{:S(2)}) async-start(bf16[16,2,8,6,96]{4,2,3,1,0:T(8,128)(2,1)} %copy.218), calls=%async_computation.8 | async-start | bytes 786432 | tf_op jit(solution)/shard_map/all_to_all | solution.py:66
  193.0 1.4 copy-start.11
  194.9 1.5 copy-start.25
  196.4 11.9 %all-to-all-start.10 = ((bf16[6,96,128]{2,0,1:T(8,128)(2,1)}), bf16[6,96,128]{2,0,1:T(8,128)(2,1)S(1)}, u32[]{:S(2)}, u32[]{:S(2)}) async-start(bf16[6,96,128]{2,0,1:T(8,128)(2,1)} %copy.228), calls=%async_computation.10 | async-start | bytes 393216 | tf_op jit(solution)/shard_map/all_to_all | solution.py:321
  200.2 1.6 copy-start.51
  200.2 2.4 copy-start.46
  209.8 1.8 copy-start.72
  209.8 1.8 copy-start.17
  209.8 2.3 copy-start.2
  209.8 2.3 copy-start.26
  211.5 1.1 copy-start.37
  211.6 1.1 copy-start.28
  211.6 1.1 copy-start.32
  211.8 1.2 copy-start.36
  212.1 1.0 copy-start.30
  212.1 1.0 copy-start.41
  231.0 4.7 %copy-start.3 = (bf16[64,6,256]{2,0,1:T(8,128)(2,1)S(1)}, bf16[64,6,256]{2,0,1:T(8,128)(2,1)}, u32[]{:S(2)}) copy-start(bf16[64,6,256]{2,0,1:T(8,128)(2,1)} %param.10) | copy-start | bytes 589828
  231.0 4.7 %copy-start.50 = (bf16[256,64]{0,1:T(8,128)(2,1)S(1)}, bf16[256,64]{0,1:T(8,128)(2,1)}, u32[]{:S(2)}) copy-start(bf16[256,64]{0,1:T(8,128)(2,1)} %param.11) | copy-start | bytes 98308
  231.0 4.7 %copy-start.57 = (f32[64,6]{0,1:T(8,128)S(1)}, f32[64,6]{0,1:T(8,128)}, u32[]{:S(2)}) copy-start(f32[64,6]{0,1:T(8,128)} %copy-done.56) | copy-start | bytes 4612
  231.0 4.7 %copy-start.65 = (f32[64,6]{0,1:T(8,128)S(1)}, f32[64,6]{0,1:T(8,128)}, u32[]{:S(2)}) copy-start(f32[64,6]{0,1:T(8,128)} %copy-done.64) | copy-start | bytes 4612
  232.1 16.2 %all-to-all-start.12 = ((bf16[16,176,128]{2,1,0:T(8,128)(2,1)}), bf16[16,176,128]{2,1,0:T(8,128)(2,1)S(1)}, u32[]{:S(2)}, u32[]{:S(2)}) async-start(bf16[16,176,128]{2,1,0:T(8,128)(2,1)} %broadcast_in_dim.8), calls=%async_computation.12 | async-start | bytes 1441792 | tf_op jit(solution)/shard_map/all_to_all | solution.py:62
  (16 other events, 11.8 us)
where the time goes:
time: 257 us; the launch traced here: 255 us
  blocking collectives  80.6 us (31%)
  local copies, waits for them, and re-layouts  50.1 us (19%)
  waiting for transfers between devices  39.7 us (15%)
  starting transfers between devices  37.9 us (15%)
  matrix products  22.9 us (9%)
  other arithmetic  21.7 us (8%)
    all_to_all x6, blocking collectives, exchanged(): lax.all_to_all(values, 'dap', split_axis=0, concat_axis=0, tiled=True)  80.6 us
    all_to_all x3, waiting for transfers between devices, gathered(): lax.all_to_all(copies, 'dap', 0, 0, tiled=True)  23.9 us
    all_to_all x3, starting transfers between devices, exchanged(): lax.all_to_all(values, 'dap', split_axis=0, concat_axis=0, tiled=True)  17.9 us
    all_to_all x3, starting transfers between devices, gathered(): lax.all_to_all(copies, 'dap', 0, 0, tiled=True)  16.2 us
    unnamed x156, local copies, waits for them, and re-layouts  15.8 us
    all_to_all x3, waiting for transfers between devices, exchanged(): lax.all_to_all(values, 'dap', split_axis=0, concat_axis=0, tiled=True)  12.8 us
    optimization_barrier x15, local copies, waits for them, and re-layouts, truncated_numbers(): return lax.optimization_barrier(values.astype(jnp.bfloat16))  9.37 us
    convert_element_type x13, other arithmetic, truncated_numbers(): return lax.optimization_barrier(values.astype(jnp.bfloat16))  7.83 us
  transfers between devices with their start and end apart: 7, of which 6 were waited for; matrix products, arithmetic and copies ran while one was open for 13% of the time, Pallas kernels for 0%

commit v1 on v0

--- a/solution.py
+++ b/solution.py
@@ -318,8 +318,11 @@
             / alignment_depth
         )
         outer_grads.append(adjoint_tensor_mean)
-    pair_columns = lax.all_to_all(
-        edge_embedding_adjoint, "dap", split_axis=1, concat_axis=0, tiled=True
+    pair_columns = jnp.concatenate(
+        lax.all_to_all(
+            jnp.stack(jnp.split(edge_embedding_adjoint, lax.axis_size("dap"), axis=1)), "dap", 0, 0
+        ),
+        axis=0,
     )
     left_all = gathered(tensor_source_factor, 1).reshape(
         alignment_depth, residues, contraction_extent

time: 257 us -> 266 us (1.035)
  local copies, waits for them, and re-layouts: 50.1 us -> 59 us
    unnamed x156 -> x171, local copies, waits for them, and re-layouts: 15.8 us -> 25 us
    optimization_barrier x15 -> x14, local copies, waits for them, and re-layouts: 9.37 us -> 8.62 us  [truncated_numbers(): return lax.optimization_barrier(values.astype(jnp.bfloat16))]
where the time goes in v1:
time: 266 us; the launch traced here: 264 us
  blocking collectives  80.6 us (30%)
  local copies, waits for them, and re-layouts  59 us (22%)
  waiting for transfers between devices  39.7 us (15%)
  starting transfers between devices  37.9 us (14%)
  matrix products  22.9 us (9%)
  other arithmetic  21.7 us (8%)
    all_to_all x6, blocking collectives, exchanged(): lax.all_to_all(values, 'dap', split_axis=0, concat_axis=0, tiled=True)  80.6 us
    unnamed x171, local copies, waits for them, and re-layouts  25 us
    all_to_all x3, waiting for transfers between devices, gathered(): lax.all_to_all(copies, 'dap', 0, 0, tiled=True)  23.9 us
    all_to_all x3, starting transfers between devices, exchanged(): lax.all_to_all(values, 'dap', split_axis=0, concat_axis=0, tiled=True)  17.9 us
    all_to_all x3, starting transfers between devices, gathered(): lax.all_to_all(copies, 'dap', 0, 0, tiled=True)  16.2 us
    all_to_all x3, waiting for transfers between devices, exchanged(): lax.all_to_all(values, 'dap', split_axis=0, concat_axis=0, tiled=True)  12.8 us
    optimization_barrier x14, local copies, waits for them, and re-layouts, truncated_numbers(): return lax.optimization_barrier(values.astype(jnp.bfloat16))  8.62 us
    convert_element_type x13, other arithmetic, truncated_numbers(): return lax.optimization_barrier(values.astype(jnp.bfloat16))  7.83 us
  transfers between devices with their start and end apart: 7, of which 6 were waited for; matrix products, arithmetic and copies ran while one was open for 13% of the time, Pallas kernels for 0%

profile of v1, /device:TPU:0, one launch (start us, length us, event | category | flops | bytes accessed | tf_op | source)
XLA Modules:
  0.0 263.9 jit_solution(870402508152713311)
XLA Ops:
  0.7 1.1 convert_reduce_fusion
  1.8 1.2 fusion.53
  3.0 1.1 fusion.48
  4.1 1.0 convolution_convert_fusion.8
  5.3 1.3 reshape.293
  6.6 8.3 %all-to-all-start = ((bf16[16,2,6144]{2,1,0:T(2,128)(2,1)}), bf16[16,2,6144]{2,1,0:T(2,128)(2,1)S(1)}, u32[]{:S(2)}, u32[]{:S(2)}) async-start(bf16[16,2,6144]{2,1,0:T(2,128)(2,1)} %reshape.293), calls=%async_computation | async-start | bytes 786432 | tf_op jit(solution)/shard_map/all_to_all | solution.py:62
  14.9 12.6 %all-to-all-done = bf16[16,2,6144]{2,1,0:T(2,128)(2,1)S(1)} async-done(((bf16[16,2,6144]{2,1,0:T(2,128)(2,1)}), bf16[16,2,6144]{2,1,0:T(2,128)(2,1)S(1)}, u32[]{:S(2)}, u32[]{:S(2)}) %all-to-all-start) | async-done | bytes 393248 | tf_op jit(solution)/shard_map/all_to_all | solution.py:62
  28.1 0.8 fusion.2
  28.9 1.0 copy.169
  32.4 15.4 %all_to_all.65 = bf16[16,2,8,6,96]{4,2,3,1,0:T(8,128)(2,1)S(1)} all-to-all(bf16[16,2,8,6,96]{4,2,3,1,0:T(8,128)(2,1)S(1)} %copy.173), channel_id=1, replica_groups=mesh['dap'=16,'dp'=2] {'dap'}, dimensions={0} | all-to-all | bytes 589824 | tf_op jit(solution)/shard_map/all_to_all | solution.py:66
  48.5 11.5 %all_to_all.66 = bf16[16,1,8,6,96]{4,2,3,1,0:T(8,128)(2,1)S(1)} all-to-all(bf16[16,1,8,6,96]{4,2,3,1,0:T(8,128)(2,1)S(1)} %bitcast.397), channel_id=1, replica_groups=mesh['dap'=16,'dp'=2] {'dap'}, dimensions={0} | all-to-all | bytes 294912 | tf_op jit(solution)/shard_map/all_to_all | solution.py:66
  61.5 1.8 fusion.74
  65.8 0.9 multiply_convert_fusion.14
  66.7 1.7 copy.183
  68.4 1.7 copy.182
  70.1 1.1 pad_maximum_fusion.3
  71.3 13.2 %all_to_all.67 = bf16[16,2,8,6,96]{4,2,3,1,0:T(8,128)(2,1)S(1)} all-to-all(bf16[16,2,8,6,96]{4,2,3,1,0:T(8,128)(2,1)S(1)} %copy.184), channel_id=1, replica_groups=mesh['dap'=16,'dp'=2] {'dap'}, dimensions={0} | all-to-all | bytes 589824 | tf_op jit(solution)/shard_map/all_to_all | solution.py:66
  85.3 11.8 %all_to_all.68 = bf16[16,1,8,6,96]{4,2,3,1,0:T(8,128)(2,1)S(1)} all-to-all(bf16[16,1,8,6,96]{4,2,3,1,0:T(8,128)(2,1)S(1)} %bitcast.398), channel_id=1, replica_groups=mesh['dap'=16,'dp'=2] {'dap'}, dimensions={0} | all-to-all | bytes 294912 | tf_op jit(solution)/shard_map/all_to_all | solution.py:66
  98.5 1.9 copy.192
  100.3 1.0 convert_reduce_fusion.3
  101.3 1.0 multiply_reduce_fusion
  102.4 1.2 fusion.96
  103.6 1.0 fusion.120
  104.6 2.1 fusion.79
  107.4 1.0 multiply_convert_fusion.12
  108.4 1.7 copy.193
  110.1 1.0 copy.194
  111.1 11.1 %all_to_all.69 = bf16[16,1,8,6,96]{4,2,3,1,0:T(8,128)(2,1)S(1)} all-to-all(bf16[16,1,8,6,96]{4,2,3,1,0:T(8,128)(2,1)S(1)} %copy.194), channel_id=1, replica_groups=mesh['dap'=16,'dp'=2] {'dap'}, dimensions={0} | all-to-all | bytes 294912 | tf_op jit(solution)/shard_map/all_to_all | solution.py:66
  122.2 1.1 fusion.16
  124.7 4.4 %all-to-all-start.6 = ((bf16[16,2,8,6,96]{4,2,3,1,0:T(8,128)(2,1)}), bf16[16,2,8,6,96]{4,2,3,1,0:T(8,128)(2,1)}, u32[]{:S(2)}, u32[]{:S(2)}) async-start(bf16[16,2,8,6,96]{4,2,3,1,0:T(8,128)(2,1)} %copy.201), calls=%async_computation.6 | async-start | bytes 786432 | tf_op jit(solution)/shard_map/all_to_all | solution.py:66
  129.1 1.8 broadcast_bitcast_fusion
  130.9 2.7 %reshape.295 = bf16[16,2,6144]{2,1,0:T(2,128)(2,1)} reshape(bf16[16,6,32,64]{3,2,1,0:T(8,128)(2,1)} %broadcast_bitcast_fusion) | data formatting | bytes 786432
  133.6 4.9 %all-to-all-done.6 = bf16[16,2,8,6,96]{4,2,3,1,0:T(8,128)(2,1)} async-done(((bf16[16,2,8,6,96]{4,2,3,1,0:T(8,128)(2,1)}), bf16[16,2,8,6,96]{4,2,3,1,0:T(8,128)(2,1)}, u32[]{:S(2)}, u32[]{:S(2)}) %all-to-all-start.6) | async-done | bytes 294944 | tf_op jit(solution)/shard_map/all_to_all | solution.py:66
  138.6 4.2 %all-to-all-start.9 = ((bf16[16,2,6144]{2,1,0:T(2,128)(2,1)}), bf16[16,2,6144]{2,1,0:T(2,128)(2,1)}, u32[]{:S(2)}, u32[]{:S(2)}) async-start(bf16[16,2,6144]{2,1,0:T(2,128)(2,1)} %reshape.295), calls=%async_computation.9 | async-start | bytes 786432 | tf_op jit(solution)/shard_map/all_to_all | solution.py:62
  142.8 1.8 slice_convert_fusion.3
  145.4 1.9 copy.203
  147.2 1.8 copy.291
  149.0 1.9 copy.206
  150.9 1.3 multiply_convert_fusion.11
  153.8 1.1 multiply_convert_fusion.1
  157.4 6.9 %all-to-all-start.7 = ((bf16[16,1,8,6,96]{4,2,3,1,0:T(8,128)(2,1)}), bf16[16,1,8,6,96]{4,2,3,1,0:T(8,128)(2,1)}, u32[]{:S(2)}, u32[]{:S(2)}) async-start(bf16[16,1,8,6,96]{4,2,3,1,0:T(8,128)(2,1)} %copy.209), calls=%async_computation.7 | async-start | bytes 393216 | tf_op jit(solution)/shard_map/all_to_all | solution.py:66
  164.3 2.7 %reshape.296 = bf16[16,6,32,64]{3,2,1,0:T(8,128)(2,1)} reshape(bf16[16,2,6144]{2,1,0:T(2,128)(2,1)} %all-to-all-done.9) | data formatting | bytes 786432
  167.0 2.7 %copy.228 = bf16[64,96,32]{1,0,2:T(8,128)(2,1)} copy(bf16[64,96,32]{0,2,1:T(8,128)(2,1)} %bitcast.380) | data formatting | bytes 786432 | tf_op jit(solution)/shard_map/reshape | solution.py:327
  169.7 1.6 copy.224
  171.3 0.9 fusion.36
  172.4 1.1 copy.213
  173.5 1.1 fusion.18
  176.0 6.7 %all-to-all-start.8 = ((bf16[16,2,8,6,96]{4,2,3,1,0:T(8,128)(2,1)}), bf16[16,2,8,6,96]{4,2,3,1,0:T(8,128)(2,1)S(1)}, u32[]{:S(2)}, u32[]{:S(2)}) async-start(bf16[16,2,8,6,96]{4,2,3,1,0:T(8,128)(2,1)} %copy.216), calls=%async_computation.8 | async-start | bytes 786432 | tf_op jit(solution)/shard_map/all_to_all | solution.py:66
  183.8 0.9 fusion.32
  184.6 7.6 %all-to-all-done.8 = bf16[16,2,8,6,96]{4,2,3,1,0:T(8,128)(2,1)S(1)} async-done(((bf16[16,2,8,6,96]{4,2,3,1,0:T(8,128)(2,1)}), bf16[16,2,8,6,96]{4,2,3,1,0:T(8,128)(2,1)S(1)}, u32[]{:S(2)}, u32[]{:S(2)}) %all-to-all-start.8) | async-done | bytes 294944 | tf_op jit(solution)/shard_map/all_to_all | solution.py:66
  205.4 3.8 %all-to-all-start.10 = ((bf16[16,6,6,128]{3,2,1,0:T(8,128)(2,1)}), bf16[16,6,6,128]{3,2,1,0:T(8,128)(2,1)S(1)}, u32[]{:S(2)}, u32[]{:S(2)}) async-start(bf16[16,6,6,128]{3,2,1,0:T(8,128)(2,1)} %constant_dynamic-update-slice_fusion), calls=%async_computation.10 | async-start | bytes 393216 | tf_op jit(solution)/shard_map/all_to_all | solution.py:322
  209.2 1.6 copy.223
  211.6 2.6 fusion.28
  214.2 3.0 %all-to-all-done.10 = bf16[16,6,6,128]{3,2,1,0:T(8,128)(2,1)S(1)} async-done(((bf16[16,6,6,128]{3,2,1,0:T(8,128)(2,1)}), bf16[16,6,6,128]{3,2,1,0:T(8,128)(2,1)S(1)}, u32[]{:S(2)}, u32[]{:S(2)}) %all-to-all-start.10) | async-done | bytes 147488 | tf_op jit(solution)/shard_map/all_to_all | solution.py:322
  217.7 0.9 copy.227
  218.7 1.7 fusion.31
  222.3 17.6 %all_to_all.70 = bf16[16,176,128]{2,1,0:T(8,128)(2,1)S(1)} all-to-all(bf16[16,176,128]{2,1,0:T(8,128)(2,1)S(1)} %bitcast.381), channel_id=1, replica_groups=mesh['dap'=16,'dp'=2] {'dap'}, dimensions={0} | all-to-all | bytes 1441792 | tf_op jit(solution)/shard_map/all_to_all | solution.py:66
  240.0 1.0 broadcast_in_dim.8
  240.9 3.6 %all-to-all-start.12 = ((bf16[16,176,128]{2,1,0:T(8,128)(2,1)}), bf16[16,176,128]{2,1,0:T(8,128)(2,1)S(1)}, u32[]{:S(2)}, u32[]{:S(2)}) async-start(bf16[16,176,128]{2,1,0:T(8,128)(2,1)} %broadcast_in_dim.8), calls=%async_computation.12 | async-start | bytes 1441792 | tf_op jit(solution)/shard_map/all_to_all | solution.py:62
  245.0 1.0 fusion.52
  246.0 11.2 %all-to-all-done.12 = bf16[16,176,128]{2,1,0:T(8,128)(2,1)S(1)} async-done(((bf16[16,176,128]{2,1,0:T(8,128)(2,1)}), bf16[16,176,128]{2,1,0:T(8,128)(2,1)S(1)}, u32[]{:S(2)}, u32[]{:S(2)}) %all-to-all-start.12) | async-done | bytes 720928 | tf_op jit(solution)/shard_map/all_to_all | solution.py:62
  257.3 0.8 slice_multiply_fusion
  258.8 1.8 slice.132
  260.6 0.9 slice_multiply_fusion.3
  (271 shorter events, 38.6 us)
Async XLA Ops:
  0.6 29.3 %copy-start = (bf16[1024,128]{1,0:T(8,128)(2,1)S(1)}, bf16[1024,128]{1,0:T(8,128)(2,1)}, u32[]{:S(2)}) copy-start(bf16[1024,128]{1,0:T(8,128)(2,1)} %param.12) | copy-start | bytes 786436
  1.8 3.3 %copy-start.56 = (f32[64,6]{0,1:T(8,128)}, f32[64,6]{0,1:T(8,128)S(1)}, u32[]{:S(2)}) copy-start(f32[64,6]{0,1:T(8,128)S(1)} %broadcast_multiply_fusion.14) | copy-start | bytes 4612
  3.0 2.2 copy-start.64
  4.1 1.1 copy-start.16
  5.1 22.9 %copy-start.47 = (bf16[64,6,32]{0,2,1:T(8,128)(2,1)}, bf16[64,6,32]{0,2,1:T(8,128)(2,1)S(1)}, u32[]{:S(2)}) copy-start(bf16[64,6,32]{0,2,1:T(8,128)(2,1)S(1)} %get-tuple-element.79) | copy-start | bytes 73732
  6.6 21.0 %all-to-all-start = ((bf16[16,2,6144]{2,1,0:T(2,128)(2,1)}), bf16[16,2,6144]{2,1,0:T(2,128)(2,1)S(1)}, u32[]{:S(2)}, u32[]{:S(2)}) async-start(bf16[16,2,6144]{2,1,0:T(2,128)(2,1)} %reshape.293), calls=%async_computation | async-start | bytes 786432 | tf_op jit(solution)/shard_map/all_to_all | solution.py:62
  28.9 1.1 copy-start.48
  29.9 1.2 copy-start.1
  29.9 1.4 copy-start.44
  30.7 1.1 copy-start.58
  31.3 30.2 %copy-start.12 = (bf16[6,96,128]{2,1,0:T(8,128)(2,1)}, bf16[6,96,128]{2,1,0:T(8,128)(2,1)S(1)}, u32[]{:S(2)}) copy-start(bf16[6,96,128]{2,1,0:T(8,128)(2,1)S(1)} %fusion.58) | copy-start | bytes 442372
  47.9 12.2 %copy-start.18 = (bf16[16,1,8,6,96]{4,2,3,1,0:T(8,128)(2,1)}, bf16[16,1,8,6,96]{4,2,3,1,0:T(8,128)(2,1)S(1)}, u32[]{:S(2)}) copy-start(bf16[16,1,8,6,96]{4,2,3,1,0:T(8,128)(2,1)S(1)} %get-tuple-element.78) | copy-start | bytes 442372
  48.1 13.2 %copy-start.54 = (bf16[128,128]{1,0:T(8,128)(2,1)S(1)}, bf16[128,128]{1,0:T(8,128)(2,1)}, u32[]{:S(2)}) copy-start(bf16[128,128]{1,0:T(8,128)(2,1)} %param.14) | copy-start | bytes 98308
  60.2 3.0 %copy-start.4 = (f32[128,6,96]{0,2,1:T(8,128)}, f32[128,6,96]{0,2,1:T(8,128)S(1)}, u32[]{:S(2)}) copy-start(f32[128,6,96]{0,2,1:T(8,128)S(1)} %copy.181) | copy-start | bytes 884740
  60.3 3.4 %copy-start.60 = (f32[6,96]{1,0:T(8,128)}, f32[6,96]{1,0:T(8,128)S(1)}, u32[]{:S(2)}) copy-start(f32[6,96]{1,0:T(8,128)S(1)} %broadcast_multiply_fusion.10) | copy-start | bytes 6916
  60.4 3.3 %copy-start.68 = (f32[6,96]{1,0:T(8,128)}, f32[6,96]{1,0:T(8,128)S(1)}, u32[]{:S(2)}) copy-start(f32[6,96]{1,0:T(8,128)S(1)} %add_rsqrt_fusion.2) | copy-start | bytes 6916
  61.3 4.2 %copy-start.42 = (bf16[128,640]{1,0:T(8,128)(2,1)S(1)}, bf16[128,640]{1,0:T(8,128)(2,1)}, u32[]{:S(2)}) copy-start(bf16[128,640]{1,0:T(8,128)(2,1)} %param.15) | copy-start | bytes 491524
  61.5 2.3 copy-start.33
  102.3 4.3 %copy-start.6 = (f32[128,6,96]{0,2,1:T(8,128)S(1)}, f32[128,6,96]{0,2,1:T(8,128)}, u32[]{:S(2)}) copy-start(f32[128,6,96]{0,2,1:T(8,128)} %copy.192) | copy-start | bytes 884740
  102.4 4.3 %copy-start.53 = (bf16[128,128]{1,0:T(8,128)(2,1)S(1)}, bf16[128,128]{1,0:T(8,128)(2,1)}, u32[]{:S(2)}) copy-start(bf16[128,128]{1,0:T(8,128)(2,1)} %param.16) | copy-start | bytes 98308
  103.6 3.6 %copy-start.29 = (bf16[128,6,96]{0,2,1:T(8,128)(2,1)}, bf16[128,6,96]{0,2,1:T(8,128)(2,1)S(1)}, u32[]{:S(2)}) copy-start(bf16[128,6,96]{0,2,1:T(8,128)(2,1)S(1)} %fusion.96) | copy-start | bytes 442372
  110.1 13.3 %copy-start.22 = (bf16[16,1,8,6,96]{4,2,3,1,0:T(8,128)(2,1)S(1)}, bf16[16,1,8,6,96]{4,2,3,1,0:T(8,128)(2,1)}, u32[]{:S(2)}) copy-start(bf16[16,1,8,6,96]{4,2,3,1,0:T(8,128)(2,1)} %copy-done.21) | copy-start | bytes 442372
  124.7 13.9 %all-to-all-start.6 = ((bf16[16,2,8,6,96]{4,2,3,1,0:T(8,128)(2,1)}), bf16[16,2,8,6,96]{4,2,3,1,0:T(8,128)(2,1)}, u32[]{:S(2)}, u32[]{:S(2)}) async-start(bf16[16,2,8,6,96]{4,2,3,1,0:T(8,128)(2,1)} %copy.201), calls=%async_computation.6 | async-start | bytes 786432 | tf_op jit(solution)/shard_map/all_to_all | solution.py:66
  138.6 18.8 %all-to-all-start.9 = ((bf16[16,2,6144]{2,1,0:T(2,128)(2,1)}), bf16[16,2,6144]{2,1,0:T(2,128)(2,1)}, u32[]{:S(2)}, u32[]{:S(2)}) async-start(bf16[16,2,6144]{2,1,0:T(2,128)(2,1)} %reshape.295), calls=%async_computation.9 | async-start | bytes 786432 | tf_op jit(solution)/shard_map/all_to_all | solution.py:62
  150.9 1.5 copy-start.43
  152.2 1.0 copy-start.38
  152.2 1.0 copy-start.63
  152.2 1.0 copy-start.71
  152.3 1.5 copy-start.34
  152.3 1.5 copy-start.35
  152.3 1.5 copy-start.49
  153.2 2.4 copy-start.5
  153.2 2.4 copy-start.55
  153.2 2.4 copy-start.61
  153.2 2.4 copy-start.69
  155.6 11.4 %copy-start.31 = (bf16[6,96,128]{2,1,0:T(8,128)(2,1)}, bf16[6,96,128]{2,1,0:T(8,128)(2,1)S(1)}, u32[]{:S(2)}) copy-start(bf16[6,96,128]{2,1,0:T(8,128)(2,1)S(1)} %multiply_convert_fusion.7) | copy-start | bytes 442372
  157.4 15.0 %all-to-all-start.7 = ((bf16[16,1,8,6,96]{4,2,3,1,0:T(8,128)(2,1)}), bf16[16,1,8,6,96]{4,2,3,1,0:T(8,128)(2,1)}, u32[]{:S(2)}, u32[]{:S(2)}) async-start(bf16[16,1,8,6,96]{4,2,3,1,0:T(8,128)(2,1)} %copy.209), calls=%async_computation.7 | async-start | bytes 393216 | tf_op jit(solution)/shard_map/all_to_all | solution.py:66
  167.0 4.4 %copy-start.15 = (bf16[6,96,128]{2,1,0:T(8,128)(2,1)S(1)}, bf16[6,96,128]{2,1,0:T(8,128)(2,1)}, u32[]{:S(2)}) copy-start(bf16[6,96,128]{2,1,0:T(8,128)(2,1)} %copy-done.14) | copy-start | bytes 442372
  167.0 4.4 %copy-start.39 = (bf16[6,96,128]{2,1,0:T(8,128)(2,1)S(1)}, bf16[6,96,128]{2,1,0:T(8,128)(2,1)}, u32[]{:S(2)}) copy-start(bf16[6,96,128]{2,1,0:T(8,128)(2,1)} %get-tuple-element.68) | copy-start | bytes 442372
  169.7 4.9 %copy-start.19 = (bf16[16,1,8,6,96]{4,2,3,1,0:T(8,128)(2,1)S(1)}, bf16[16,1,8,6,96]{4,2,3,1,0:T(8,128)(2,1)}, u32[]{:S(2)}) copy-start(bf16[16,1,8,6,96]{4,2,3,1,0:T(8,128)(2,1)} %copy-done.18) | copy-start | bytes 442372
  175.1 7.9 %copy-start.52 = (bf16[128,128]{1,0:T(8,128)(2,1)S(1)}, bf16[128,128]{1,0:T(8,128)(2,1)}, u32[]{:S(2)}) copy-start(bf16[128,128]{1,0:T(8,128)(2,1)} %fusion.36) | copy-start | bytes 98308
  175.2 8.6 %copy-start.13 = (bf16[6,96,128]{2,1,0:T(8,128)(2,1)S(1)}, bf16[6,96,128]{2,1,0:T(8,128)(2,1)}, u32[]{:S(2)}) copy-start(bf16[6,96,128]{2,1,0:T(8,128)(2,1)} %copy-done.12) | copy-start | bytes 442372
  175.2 8.6 %copy-start.26 = (bf16[6,96,128]{2,1,0:T(8,128)(2,1)S(1)}, bf16[6,96,128]{2,1,0:T(8,128)(2,1)}, u32[]{:S(2)}) copy-start(bf16[6,96,128]{2,1,0:T(8,128)(2,1)} %get-tuple-element.46) | copy-start | bytes 442372
  176.0 16.3 %all-to-all-start.8 = ((bf16[16,2,8,6,96]{4,2,3,1,0:T(8,128)(2,1)}), bf16[16,2,8,6,96]{4,2,3,1,0:T(8,128)(2,1)S(1)}, u32[]{:S(2)}, u32[]{:S(2)}) async-start(bf16[16,2,8,6,96]{4,2,3,1,0:T(8,128)(2,1)} %copy.216), calls=%async_computation.8 | async-start | bytes 786432 | tf_op jit(solution)/shard_map/all_to_all | solution.py:66
  193.0 1.4 copy-start.11
  194.9 10.5 %copy-start.24 = (bf16[6,96,128]{2,1,0:T(8,128)(2,1)}, bf16[6,96,128]{2,1,0:T(8,128)(2,1)S(1)}, u32[]{:S(2)}) copy-start(bf16[6,96,128]{2,1,0:T(8,128)(2,1)S(1)} %fusion.72) | copy-start | bytes 442372
  205.4 11.9 %all-to-all-start.10 = ((bf16[16,6,6,128]{3,2,1,0:T(8,128)(2,1)}), bf16[16,6,6,128]{3,2,1,0:T(8,128)(2,1)S(1)}, u32[]{:S(2)}, u32[]{:S(2)}) async-start(bf16[16,6,6,128]{3,2,1,0:T(8,128)(2,1)} %constant_dynamic-update-slice_fusion), calls=%async_computation.10 | async-start | bytes 393216 | tf_op jit(solution)/shard_map/all_to_all | solution.py:322
  209.2 1.6 copy-start.51
  209.2 2.4 copy-start.46
  218.6 1.8 copy-start.72
  218.6 1.8 copy-start.17
  218.6 2.3 copy-start.2
  218.6 2.3 copy-start.25
  220.4 1.1 copy-start.37
  220.5 1.1 copy-start.28
  220.5 1.1 copy-start.32
  220.7 1.1 copy-start.36
  221.0 1.0 copy-start.30
  221.0 1.0 copy-start.41
  239.9 4.7 %copy-start.3 = (bf16[64,6,256]{2,0,1:T(8,128)(2,1)S(1)}, bf16[64,6,256]{2,0,1:T(8,128)(2,1)}, u32[]{:S(2)}) copy-start(bf16[64,6,256]{2,0,1:T(8,128)(2,1)} %param.10) | copy-start | bytes 589828
  239.9 4.7 %copy-start.50 = (bf16[256,64]{0,1:T(8,128)(2,1)S(1)}, bf16[256,64]{0,1:T(8,128)(2,1)}, u32[]{:S(2)}) copy-start(bf16[256,64]{0,1:T(8,128)(2,1)} %param.11) | copy-start | bytes 98308
  239.9 4.7 %copy-start.57 = (f32[64,6]{0,1:T(8,128)S(1)}, f32[64,6]{0,1:T(8,128)}, u32[]{:S(2)}) copy-start(f32[64,6]{0,1:T(8,128)} %copy-done.56) | copy-start | bytes 4612
  239.9 4.7 %copy-start.65 = (f32[64,6]{0,1:T(8,128)S(1)}, f32[64,6]{0,1:T(8,128)}, u32[]{:S(2)}) copy-start(f32[64,6]{0,1:T(8,128)} %copy-done.64) | copy-start | bytes 4612
  240.9 16.2 %all-to-all-start.12 = ((bf16[16,176,128]{2,1,0:T(8,128)(2,1)}), bf16[16,176,128]{2,1,0:T(8,128)(2,1)S(1)}, u32[]{:S(2)}, u32[]{:S(2)}) async-start(bf16[16,176,128]{2,1,0:T(8,128)(2,1)} %broadcast_in_dim.8), calls=%async_computation.12 | async-start | bytes 1441792 | tf_op jit(solution)/shard_map/all_to_all | solution.py:62
  (16 other events, 11.8 us)
